TPU v7x, 32 devices: a whole 2x2x4 slice. The times are simulated.
32 devices in a mesh: dp: 8 (over z, y), owner: 4 (over x, core).
Axes of the slice: x: 2, y: 2, z: 4, core: 2. Of those that a mesh axis runs over, the one named last changes fastest.
Arguments:
- grads: float32 [8, 32, 512, 128], P('dp', None, 'owner'), may hold values from -21 to 21
- momentum: float32 [64, 512, 128], P('dp', 'owner'), may hold values from -30 to 30
- slot_matrix: int32 [64], replicated, may hold values from -1 to 31, as said below
Outputs:
- updates: bfloat16 [32, 512, 128], P(None, 'owner')
- momentum_out: float32 [64, 512, 128], P('dp', 'owner')
Inputs may be any that keep to these rules, and one draw needn't show every extreme that they name: `slot_matrix`: entry s names the block held by slot s, or is -1 if slot s is empty; slots s with s // 8 == g belong to the owner group at index g of dp. Every one of the 32 blocks is held by exactly one slot, and some group, drawn from the seed, has all 8 slots filled.
All inputs are finite; a program needn't handle non-finite values.
Results may differ from a plain program's by a relative error of at most 0.038.
Values may be sent and summed in bfloat16 or wider, within the bound.
A program may use at most 64 MiB of HBM per device.

v0:
```python
import math

import jax
import jax.numpy as jnp
from jax import lax
from jax.sharding import PartitionSpec as P

C = 512
ITERS = 5


momentum_rate = 0.95
epsilon_norm = 1e-07
first_coef = 3.4445
third_coef = -4.775
fifth_coef = 2.0315


def local_gram(iterate):
    return jnp.einsum("kcr,kcq->krq", iterate, iterate, preferred_element_type=jnp.float32)


def make_poly(gram_matrix):
    square = jnp.einsum(
        "krq,kqp->krp", gram_matrix, gram_matrix, preferred_element_type=jnp.float32
    )
    return (third_coef * gram_matrix.astype(jnp.float32) + fifth_coef * square).astype(jnp.bfloat16)


def advance(iterate, polynomial):
    product = jnp.einsum("kcr,krq->kcq", iterate, polynomial, preferred_element_type=jnp.float32)
    return first_coef * iterate.astype(jnp.float32) + product


def whole_sweeps(iterate):
    for iteration in range(ITERS - 1):
        polynomial = make_poly(local_gram(iterate).astype(jnp.bfloat16))
        iterate = advance(iterate, polynomial).astype(jnp.bfloat16)
    return (iterate, make_poly(local_gram(iterate).astype(jnp.bfloat16)))


def finish(iterate, polynomial):
    return (math.sqrt(C) * advance(iterate, polynomial)).astype(jnp.bfloat16)


def local(grads, momentum, slot_matrix):
    partial_value = grads[0]
    present = (slot_matrix >= 0).astype(jnp.float32)
    picked = jnp.take(partial_value, jnp.maximum(slot_matrix, 0), axis=0) * present[:, None, None]
    summed = lax.psum_scatter(picked, "dp", scatter_dimension=0, tiled=True)
    renewed = momentum_rate * momentum + summed
    squares = lax.psum(jnp.sum(renewed * renewed, axis=(1, 2)), "owner")
    initial = (renewed / (jnp.sqrt(squares) + epsilon_norm)[:, None, None]).astype(jnp.bfloat16)
    iterate, polynomial = whole_sweeps(
        lax.all_to_all(initial, "owner", split_axis=0, concat_axis=1, tiled=True)
    )
    spread = finish(iterate, polynomial)
    update = lax.all_to_all(spread, "owner", split_axis=1, concat_axis=0, tiled=True)
    everyone = lax.all_gather(update, "dp", axis=0, tiled=True)
    all_slots = everyone.shape[0]
    matches = slot_matrix[None, :] == jnp.arange(grads.shape[1], dtype=jnp.int32)[:, None]
    slot_of = jnp.sum(
        jnp.where(matches, jnp.arange(all_slots, dtype=jnp.int32)[None, :], 0), axis=1
    )
    return (jnp.take(everyone, slot_of, axis=0), renewed)


def solution(mesh):
    return jax.shard_map(
        local,
        mesh=mesh,
        in_specs=(P("dp", None, "owner", None), P("dp", "owner", None), P()),
        out_specs=(P(None, "owner", None), P("dp", "owner", None)),
        check_vma=False,
    )
```

profile of v0, /device:TPU:0, one launch (start us, length us, event | category | flops | bytes accessed | tf_op | source)
XLA Modules:
  0.0 194.9 jit_solution(15638819623874804117)
XLA Ops:
  7.2 0.8 broadcast_compare_fusion
  8.0 0.7 broadcast_maximum_fusion
  8.8 2.8 %gather_fusion = f32[64,128,128]{2,1,0:T(8,128)} fusion(f32[32,128,128]{2,1,0:T(8,128)S(1)} %bitcast.38, s32[1024]{0:T(1024)S(1)} %pad_clamp_fusion.1), kind=kCustom, calls=%fused_computation | custom fusion | bytes 8388864 | tf_op jit(solution)/shard_map/jit(_take)/gather | solution.py:49
  11.5 4.6 %select_multiply_fusion = f32[64,128,128]{2,1,0:T(8,128)} fusion(f32[64,128,128]{2,1,0:T(8,128)} %gather_fusion, f32[64]{0:T(128)S(1)} %get-tuple-element.5, pred[64]{0:T(512)(128)(4,1)S(1)} %get-tuple-element.4), kind=kLoop, calls=%fused_computation.2 | loop fusion | flops 2097152 | bytes 8388928 | tf_op jit(solution)/shard_map/mul | solution.py:49
  16.2 91.1 %reduce-scatter.2.cloned.1.call-done = f32[8,128,128]{2,1,0:T(8,128)} async-done(((f32[64,128,128]{2,1,0:T(8,128)}), f32[8,128,128]{2,1,0:T(8,128)}) %reduce-scatter.2.cloned.1.call-update) | async-done | bytes 524304 | tf_op jit(solution)/shard_map/reduce_scatter | solution.py:50
  107.3 1.2 multiply_reduce_fusion
  108.5 6.2 %psum.7 = f32[8]{0:T(128)S(1)} all-reduce(f32[8]{0:T(128)S(1)} %get-tuple-element.2), channel_id=1, replica_groups=mesh['dp'=8,'owner'=4] {'owner'}, use_global_device_ids=true, to_apply=%region_3.4 | all-reduce | flops 8 | bytes 64 | tf_op jit(solution)/shard_map/psum | solution.py:52
  114.8 8.4 %all_to_all.36 = bf16[8,128,128]{2,1,0:T(8,128)(2,1)S(1)} all-to-all(bf16[8,128,128]{2,1,0:T(8,128)(2,1)S(1)} %divide_convert_fusion), channel_id=1, replica_groups=mesh['dp'=8,'owner'=4] {'owner'}, dimensions={0} | all-to-all | bytes 524288 | tf_op jit(solution)/shard_map/all_to_all | solution.py:55
  123.3 0.3 convolution_convert_fusion.4
  123.5 0.4 fusion.2
  123.9 0.3 convolution_convert_fusion.3
  124.2 0.4 fusion.3
  124.6 0.3 convolution_convert_fusion.2
  124.8 0.4 fusion.4
  125.2 0.3 convolution_convert_fusion.1
  125.5 0.4 fusion.5
  125.9 0.3 convolution_convert_fusion
  126.1 0.4 fusion.1
  126.5 0.3 copy.40
  126.8 8.4 %all_to_all.37 = bf16[2,512,128]{2,0,1:T(2,128)(2,1)S(1)} all-to-all(bf16[2,512,128]{2,0,1:T(2,128)(2,1)S(1)} %copy.40), channel_id=1, replica_groups=mesh['dp'=8,'owner'=4] {'owner'}, dimensions={1} | all-to-all | bytes 524288 | tf_op jit(solution)/shard_map/all_to_all | solution.py:58
  135.2 0.7 copy.42
  136.1 48.5 %all-gather.2.cloned.1.call-done = bf16[64,128,128]{2,1,0:T(8,128)(2,1)} async-done(((bf16[8,128,128]{2,1,0:T(8,128)(2,1)}), bf16[64,128,128]{2,1,0:T(8,128)(2,1)}) %all-gather.2.cloned.1.call-update) | async-done | bytes 2097168 | tf_op jit(solution)/shard_map/all_gather | solution.py:59
  184.6 2.3 %gather_fusion.1 = bf16[32,128,128]{2,1,0:T(8,128)(2,1)S(1)} fusion(bf16[64,128,128]{2,1,0:T(8,128)(2,1)} %all-gather.2.cloned.1.call-done, s32[1024]{0:T(1024)S(1)} %pad_clamp_fusion), kind=kCustom, calls=%fused_computation.1 | custom fusion | bytes 2097280 | tf_op jit(solution)/shard_map/jit(_take)/gather | solution.py:65
  186.9 1.1 broadcast_select_fusion
  (21 shorter events, 0.5 us)
Async XLA Ops:
  7.2 1.6 copy-start
  7.2 100.1 %reduce-scatter.2.cloned.1.call-start = ((), (), s32[]{:S(2)}) async-start(), calls=%async_computation.3 | async-start | bytes 4718592 | tf_op jit(solution)/shard_map/reduce_scatter | solution.py:50
  16.1 91.2 %copy-start.2 = (f32[8,128,128]{2,1,0:T(8,128)S(1)}, f32[8,128,128]{2,1,0:T(8,128)}, u32[]{:S(2)}) copy-start(f32[8,128,128]{2,1,0:T(8,128)} %param.4) | copy-start | bytes 1572868
  16.1 168.5 %all-gather.2.cloned.1.call-start = ((), (), s32[]{:S(2)}) async-start(), calls=%async_computation.4 | async-start | bytes 2359296 | tf_op jit(solution)/shard_map/all_gather | solution.py:59
  108.5 14.7 %copy-start.1 = (f32[8,128,128]{2,1,0:T(8,128)}, f32[8,128,128]{2,1,0:T(8,128)S(1)}, u32[]{:S(2)}) copy-start(f32[8,128,128]{2,1,0:T(8,128)S(1)} %get-tuple-element.3) | copy-start | bytes 1572868
  123.5 12.4 %copy-start.3 = (s32[64]{0:T(128)S(1)}, s32[64]{0:T(128)}, u32[]{:S(2)}) copy-start(s32[64]{0:T(128)} %param.5) | copy-start | bytes 772
Sparse Core Ops, SparseCore 0:
  16.2 91.0 reduce-scatter.1
  136.1 48.4 all-gather.1
where the time goes:
time: 195 us
  waiting for transfers between devices  140 us (72%)
  blocking collectives  23 us (12%)
  between operations  14.2 us (7%)
  other arithmetic  8.63 us (4%)
  local copies, waits for them, and re-layouts  6.24 us (3%)
  matrix products  3.19 us (2%)
    reduce_scatter x1, waiting for transfers between devices, local(): summed = lax.psum_scatter(picked, 'dp', scatter_dimension=0, tiled=True)  91.1 us
    all_gather x1, waiting for transfers between devices, local(): everyone = lax.all_gather(update, 'dp', axis=0, tiled=True)  48.5 us
    all_to_all x1, blocking collectives, local(): lax.all_to_all(initial, 'owner', split_axis=0, concat_axis=1, tiled=True)  8.39 us
    all_to_all x1, blocking collectives, local(): lax.all_to_all(spread, 'owner', split_axis=1, concat_axis=0, tiled=True)  8.39 us
    psum x1, blocking collectives, local(): squares = lax.psum(jnp.sum(renewed * renewed, axis=(1, 2)), 'owner')  6.2 us
    mul x1, other arithmetic, local(): jnp.take(partial_value, jnp.maximum(slot_matrix, 0), axis=0)  4.55 us
  transfers between devices with their start and end apart: 2, of which 2 were waited for; matrix products, arithmetic and copies ran while one was open for 0% of the time, Pallas kernels for 0%

commit v1 on v0

v1 whole, which is shorter than its diff:
```python
import functools
import math

import jax
import jax.numpy as jnp
from jax import lax
from jax.experimental import pallas as pl
from jax.experimental.pallas import tpu as pltpu
from jax.sharding import PartitionSpec as P

ITERS = 5

momentum_rate = 0.95
epsilon_norm = 1e-07
first_coef = 3.4445
third_coef = -4.775
fifth_coef = 2.0315

MESH = pl.DeviceIdType.MESH
F32 = jnp.float32
BF16 = jnp.bfloat16


def orthogonal(x):
    rows = x.shape[0]
    norm = jnp.sqrt(jnp.sum(x * x, axis=(0, 1), keepdims=True)) + epsilon_norm
    iterate = (x / norm).astype(BF16)
    advanced = None
    for iteration in range(ITERS):
        gram = lax.dot_general(
            iterate, iterate, (((0,), (0,)), ((), ())), preferred_element_type=F32
        ).astype(BF16)
        square = jnp.dot(gram, gram, preferred_element_type=F32)
        poly = (third_coef * gram.astype(F32) + fifth_coef * square).astype(BF16)
        advanced = first_coef * iterate.astype(F32) + jnp.dot(
            iterate, poly, preferred_element_type=F32
        )
        iterate = advanced.astype(BF16)
    return (math.sqrt(rows) * advanced).astype(BF16)


def kernel(
    n_dp, n_ow, per, workers,
    slots_ref, grads_ref, mom_ref, upd_ref, momout_ref,
    ypack, yrecv, zsend, zrecv, own, held, orecv, ubuf, every, ysel, yselrecv,
    ys, yr, zs, zr, os_, or_, ms, mr, qs, qr, us, ur, vs, vr, ws, wr,
):
    n_z = n_dp // 2
    mats = grads_ref.shape[0]
    nb = mats // n_dp
    n_slots = mom_ref.shape[0]
    dp = lax.axis_index("dp")
    ow = lax.axis_index("owner")
    z = lax.div(dp, 2)
    y = lax.rem(dp, 2)
    other = 2 * z + 1 - y

    def up(t):
        return lax.rem(z + 1 + t, n_z)

    def down(t):
        return lax.rem(z - 1 - t + 2 * n_z, n_z)

    def owner_at(t):
        return lax.rem(ow + t, n_ow)

    def owner_from(t):
        return lax.rem(ow - t + n_ow, n_ow)

    def remote(src, dst, send, recv, to):
        return pltpu.make_async_remote_copy(
            src_ref=src, dst_ref=dst, send_sem=send, recv_sem=recv,
            device_id=to, device_id_type=MESH,
        )

    barrier = pltpu.get_barrier_semaphore()
    pl.semaphore_signal(barrier, inc=1, device_id=(other, ow), device_id_type=MESH)
    for t in range(n_z - 1):
        pl.semaphore_signal(barrier, inc=1, device_id=(2 * up(t) + y, ow), device_id_type=MESH)
    for t in range(1, n_ow):
        pl.semaphore_signal(barrier, inc=1, device_id=(dp, owner_at(t)), device_id_type=MESH)

    held_slots = [slots_ref[dp * n_slots + k] for k in range(n_slots)]

    def partial(m):
        place = jnp.int32(0)
        weight = F32(0.0)
        for k in range(n_slots):
            hit = held_slots[k] == m
            place = jnp.where(hit, k, place)
            weight = jnp.where(hit, F32(momentum_rate), weight)
        return grads_ref[m] + weight * mom_ref[place]

    y_copies = []
    for t in range(n_z):
        def pack(j, carry, t=t):
            ypack[t, j] = partial((2 * up(t) + 1 - y) * nb + j).astype(BF16)
            return carry
        lax.fori_loop(0, nb, pack, 0)
        if t == 0:
            pl.semaphore_wait(barrier, 1 + (n_z - 1) + (n_ow - 1))
        copy = remote(ypack.at[t], yrecv.at[t], ys.at[t], yr.at[t], (other, ow))
        copy.start()
        y_copies.append(copy)

    z_copies = []
    for t in range(n_z):
        y_copies[t].wait_recv()
        def add(j, carry, t=t):
            value = partial((2 * up(t) + y) * nb + j) + yrecv[t, j].astype(F32)
            if t < n_z - 1:
                zsend[t, j] = value.astype(BF16)
            else:
                own[j] = value
            return carry
        lax.fori_loop(0, nb, add, 0)
        if t < n_z - 1:
            copy = remote(zsend.at[t], zrecv.at[t], zs.at[t], zr.at[t], (2 * up(t) + y, ow))
            copy.start()
            z_copies.append(copy)

    for copy in z_copies:
        copy.wait_recv()

    mine = pl.ds(z * nb, nb)

    def total(j, carry):
        value = own[j]
        for t in range(n_z - 1):
            value = value + zrecv[t, j].astype(F32)
        held[z * nb + j] = value.astype(BF16)
        return carry
    lax.fori_loop(0, nb, total, 0)

    def when_worker(index, fn):
        if workers == n_ow:
            fn()
        else:
            pl.when(index < workers)(fn)

    def share(j):
        return pl.ds(j * per, per)

    o_copies = []
    for t in range(1, n_ow):
        j = owner_at(t)
        copy = remote(
            held.at[pl.ds(z * nb + j * per, per)], orecv.at[ow],
            os_.at[t - 1], or_.at[t - 1], (dp, j),
        )
        when_worker(j, copy.start)
        o_copies.append(copy)
    m_copies = []
    for t in range(n_z - 1):
        copy = remote(held.at[mine], held.at[mine], ms.at[t], mr.at[t], (2 * up(t) + y, ow))
        copy.start()
        m_copies.append(copy)

    def keep_own():
        orecv[ow] = held[pl.ds(z * nb + ow * per, per)]
    when_worker(ow, keep_own)

    def work():
        for copy in o_copies:
            copy.wait_recv()
        for p in range(per):
            pieces = [orecv[o, p].astype(F32) for o in range(n_ow)]
            update = orthogonal(jnp.concatenate(pieces, axis=0))
            rows = update.shape[0] // n_ow
            for o in range(n_ow):
                ubuf[o, p] = update[o * rows:(o + 1) * rows]
    when_worker(ow, work)

    home = pl.ds(dp * nb + ow * per, per)
    u_copies = []
    for t in range(1, n_ow):
        j = owner_at(t)
        copy = remote(ubuf.at[j], every.at[home], us.at[t - 1], ur.at[t - 1], (dp, j))
        when_worker(ow, copy.start)
        u_copies.append(copy)

    def keep_update():
        every[home] = ubuf[ow]
    when_worker(ow, keep_update)

    for copy in m_copies:
        copy.wait_recv()

    def place_of(m):
        m = jnp.maximum(m, 0)
        return lax.div(m, 2 * nb) * nb + lax.rem(m, nb)

    def pick(k, carry):
        ysel[k] = held[place_of(slots_ref[other * n_slots + k])]
        return carry
    lax.fori_loop(0, n_slots, pick, 0)
    q_copy = remote(ysel, yselrecv, qs, qr, (other, ow))
    q_copy.start()

    for t in range(1, n_ow):
        when_worker(owner_from(t), u_copies[t - 1].wait_recv)

    def chunk(g):
        return pl.ds(g * nb, nb)

    v_copies = []
    for t in range(n_z - 1):
        copy = remote(
            every.at[chunk(dp)], every.at[chunk(dp)], vs.at[t], vr.at[t], (2 * up(t) + y, ow)
        )
        copy.start()
        v_copies.append(copy)
    w_copies = []
    copy = remote(
        every.at[chunk(dp)], every.at[chunk(dp)], ws.at[n_z - 1], wr.at[n_z - 1], (other, ow)
    )
    copy.start()
    w_copies.append(copy)
    for t in range(n_z - 1):
        v_copies[t].wait_recv()
        g = 2 * down(t) + y
        copy = remote(every.at[chunk(g)], every.at[chunk(g)], ws.at[t], wr.at[t], (other, ow))
        copy.start()
        w_copies.append(copy)

    q_copy.wait_recv()

    def renew(k, carry):
        m = slots_ref[dp * n_slots + k]
        side = lax.rem(lax.div(jnp.maximum(m, 0), nb), 2)
        local = jnp.where(side == y, F32(1.0), F32(0.0))
        present = jnp.where(m >= 0, F32(1.0), F32(0.0))
        near = held[place_of(m)].astype(F32)
        far = yselrecv[k].astype(F32)
        summed = present * (local * near + (1.0 - local) * far)
        momout_ref[k] = summed + (1.0 - present) * (F32(momentum_rate) * mom_ref[k])
        return carry
    lax.fori_loop(0, n_slots, renew, 0)

    for copy in w_copies:
        copy.wait_recv()
    upd_ref[...] = every[...]

    for copy in y_copies + z_copies + m_copies + [q_copy] + v_copies + w_copies:
        copy.wait_send()
    for t in range(1, n_ow):
        when_worker(owner_at(t), o_copies[t - 1].wait_send)
        when_worker(ow, u_copies[t - 1].wait_send)


def local(n_dp, n_ow, grads, momentum, slot_matrix):
    mats, rows, cols = grads.shape[1:]
    n_slots = momentum.shape[0]
    nb = mats // n_dp
    n_z = n_dp // 2
    workers = min(nb, n_ow)
    per = nb // workers
    block = (rows, cols)
    vmem = pl.BlockSpec(memory_space=pltpu.VMEM)
    dma = pltpu.SemaphoreType.DMA
    counts = (n_z, n_z - 1, n_ow - 1, n_z - 1, None, n_ow - 1, n_z - 1, n_z)
    sems = []
    for count in counts:
        sems += [dma if count is None else dma((count,))] * 2
    updates, renewed = pl.pallas_call(
        functools.partial(kernel, n_dp, n_ow, per, workers),
        out_shape=(
            jax.ShapeDtypeStruct((mats,) + block, BF16),
            jax.ShapeDtypeStruct(momentum.shape, F32),
        ),
        in_specs=[pl.BlockSpec(memory_space=pltpu.SMEM), vmem, vmem],
        out_specs=(vmem, vmem),
        scratch_shapes=[
            pltpu.VMEM((n_z, nb) + block, BF16),
            pltpu.VMEM((n_z, nb) + block, BF16),
            pltpu.VMEM((n_z - 1, nb) + block, BF16),
            pltpu.VMEM((n_z - 1, nb) + block, BF16),
            pltpu.VMEM((nb,) + block, F32),
            pltpu.VMEM((n_z * nb,) + block, BF16),
            pltpu.VMEM((n_ow, per) + block, BF16),
            pltpu.VMEM((n_ow, per) + block, BF16),
            pltpu.VMEM((mats,) + block, BF16),
            pltpu.VMEM((n_slots,) + block, BF16),
            pltpu.VMEM((n_slots,) + block, BF16),
        ] + sems,
        compiler_params=pltpu.CompilerParams(collective_id=0, has_side_effects=True),
    )(slot_matrix, grads[0], momentum)
    return updates, renewed


def solution(mesh):
    return jax.shard_map(
        functools.partial(local, mesh.shape["dp"], mesh.shape["owner"]),
        mesh=mesh,
        in_specs=(P("dp", None, "owner", None), P("dp", "owner", None), P()),
        out_specs=(P(None, "owner", None), P("dp", "owner", None)),
        check_vma=False,
    )
```

time: 195 us -> 59 us (0.30)
  waiting for transfers between devices: 140 us -> 0 us
  Pallas kernels: 0 us -> 54.2 us
  blocking collectives: 23 us -> 0 us
  between operations: 14.2 us -> 0.65 us
  other arithmetic: 8.63 us -> 0 us
  matrix products: 3.19 us -> 0 us
  local copies, waits for them, and re-layouts: 6.24 us -> 3.16 us
    reduce_scatter x1 -> x0, waiting for transfers between devices: 91.1 us -> none  [local(): summed = lax.psum_scatter(picked, 'dp', scatter_dimension=0, tiled=True)]
    pallas_call x0 -> x1, Pallas kernels: none -> 54.2 us  [local(): pl.pallas_call(functools.partial(kernel, n_dp, n_ow, per, workers), out_s...]
    all_gather x1 -> x0, waiting for transfers between devices: 48.5 us -> none  [local(): everyone = lax.all_gather(update, 'dp', axis=0, tiled=True)]
    all_to_all x2 -> x0, blocking collectives: 16.8 us -> none  [the longest x1 8.39 us: local(): lax.all_to_all(initial, 'owner', split_axis=0, concat_axis=1, tiled=True)]
    psum x1 -> x0, blocking collectives: 6.2 us -> none  [local(): squares = lax.psum(jnp.sum(renewed * renewed, axis=(1, 2)), 'owner')]
    gather x2 -> x0, local copies, waits for them, and re-layouts: 5.09 us -> none  [the longest x1 2.75 us: local(): jnp.take(partial_value, jnp.maximum(slot_matrix, 0), axis=0)]
    mul x1 -> x0, other arithmetic: 4.55 us -> none  [local(): jnp.take(partial_value, jnp.maximum(slot_matrix, 0), axis=0)]
    dot_general x10 -> x0, matrix products: 3.19 us -> none  [the longest x5 1.81 us: advance(): jnp.einsum('kcr,krq->kcq', iterate, polynomial, preferred_element_type=jn...]
  transfers between devices with their start and end apart: 2 -> 0, of which waited for: 2 -> 0; matrix products, arithmetic and copies ran while one was open for 0% -> 0% of each run, Pallas kernels for 0% -> 0%
where the time goes in v1:
time: 59 us; the launch traced here: 58 us
  Pallas kernels  54.2 us (92%)
  local copies, waits for them, and re-layouts  3.16 us (5%)
  between operations  0.65 us (1%)
    pallas_call x1, Pallas kernels, local(): pl.pallas_call(functools.partial(kernel, n_dp, n_ow, per, workers), out_s...  54.2 us
    unnamed x4, local copies, waits for them, and re-layouts  3.16 us

profile of v1, /device:TPU:0, one launch (start us, length us, event | category | flops | bytes accessed | tf_op | source)
XLA Modules:
  0.0 58.0 jit_solution(18115205802945882344)
XLA Ops:
  0.6 54.2 %shard_map.50 = (bf16[32,128,128]{2,1,0:T(8,128)(2,1)}, f32[8,128,128]{2,1,0:T(8,128)}) custom-call(s32[64]{0:T(128)} %slots_ref.1, f32[32,128,128]{2,1,0:T(8,128)} %bitcast.1, f32[8,128,128]{2,1,0:T(8,128)} %mom_ref.1), custom_call_target="tpu_custom_call" | custom-call | tf_op jit(solution)/shard_map/pallas_call | solution.py:265
  54.8 0.0 copy-start
  54.8 2.4 %copy.7 = bf16[32,128,128]{2,1,0:T(8,128)(2,1)} copy(bf16[32,128,128]{2,1,0:T(8,128)(2,1)} %get-tuple-element.4) | data formatting | bytes 2097152
  57.2 0.0 copy-done
  57.2 0.8 %copy.8 = f32[8,128,128]{2,1,0:T(8,128)} copy(f32[8,128,128]{2,1,0:T(8,128)S(1)} %copy-done) | data formatting | bytes 1048576
Async XLA Ops:
  54.8 2.4 %copy-start = (f32[8,128,128]{2,1,0:T(8,128)S(1)}, f32[8,128,128]{2,1,0:T(8,128)}, u32[]{:S(2)}) copy-start(f32[8,128,128]{2,1,0:T(8,128)} %get-tuple-element.5) | copy-start | bytes 1572868

commit v2 on v1

--- a/solution.py
+++ b/solution.py
@@ -21,29 +21,25 @@
 BF16 = jnp.bfloat16
 
 
-def orthogonal(x):
-    rows = x.shape[0]
+def normalized(x):
     norm = jnp.sqrt(jnp.sum(x * x, axis=(0, 1), keepdims=True)) + epsilon_norm
-    iterate = (x / norm).astype(BF16)
-    advanced = None
-    for iteration in range(ITERS):
-        gram = lax.dot_general(
-            iterate, iterate, (((0,), (0,)), ((), ())), preferred_element_type=F32
-        ).astype(BF16)
-        square = jnp.dot(gram, gram, preferred_element_type=F32)
-        poly = (third_coef * gram.astype(F32) + fifth_coef * square).astype(BF16)
-        advanced = first_coef * iterate.astype(F32) + jnp.dot(
-            iterate, poly, preferred_element_type=F32
-        )
-        iterate = advanced.astype(BF16)
-    return (math.sqrt(rows) * advanced).astype(BF16)
+    return (x / norm).astype(BF16)
+
+
+def sweep(iterate):
+    gram = lax.dot_general(
+        iterate, iterate, (((0,), (0,)), ((), ())), preferred_element_type=F32
+    ).astype(BF16)
+    square = jnp.dot(gram, gram, preferred_element_type=F32)
+    poly = (third_coef * gram.astype(F32) + fifth_coef * square).astype(BF16)
+    return first_coef * iterate.astype(F32) + jnp.dot(iterate, poly, preferred_element_type=F32)
 
 
 def kernel(
     n_dp, n_ow, per, workers,
     slots_ref, grads_ref, mom_ref, upd_ref, momout_ref,
-    ypack, yrecv, zsend, zrecv, own, held, orecv, ubuf, every, ysel, yselrecv,
-    ys, yr, zs, zr, os_, or_, ms, mr, qs, qr, us, ur, vs, vr, ws, wr,
+    ypack, yrecv, zsend, zrecv, own, held, orecv, work, ubuf, every, ysel, yselrecv,
+    ys, yr, zs, zr, os_, or_, ms, mr, qs, qr, us, ur, vs, vr, ws, wr, bs, br,
 ):
     n_z = n_dp // 2
     mats = grads_ref.shape[0]
@@ -150,26 +146,88 @@
         )
         when_worker(j, copy.start)
         o_copies.append(copy)
-    m_copies = []
-    for t in range(n_z - 1):
-        copy = remote(held.at[mine], held.at[mine], ms.at[t], mr.at[t], (2 * up(t) + y, ow))
-        copy.start()
-        m_copies.append(copy)
+    flows = ((1, z < n_z - 1), (-1, z > 0))
+
+    def within(index):
+        return jnp.logical_and(index >= 0, index < n_z)
+
+    def leg(f, k, item, region, buf, send, recv):
+        step, open_ahead = flows[f]
+        chunk = z - step * k
+        where = region(chunk)
+        to = jnp.clip(z + step, 0, n_z - 1)
+        copy = remote(
+            buf.at[where], buf.at[where], send.at[f, k, item], recv.at[f, k, item],
+            (2 * to + y, ow),
+        )
+        sends = jnp.logical_and(open_ahead, within(chunk))
+        takes = within(chunk - step)
+        return copy, sends, takes
+
+    pending = []
+
+    def launch(legs, k, item):
+        for f in range(2):
+            copy, sends, _ = legs(f, k, item)
+            pl.when(sends)(copy.start)
+            pending.append((copy, sends))
+
+    def arrive(legs, k, item):
+        for f in range(2):
+            copy, _, takes = legs(f, k, item)
+            pl.when(takes)(copy.wait_recv)
+
+    half = nb // 2
+    parts = ((0, half), (half, nb - half))
+
+    def m_legs(f, k, item):
+        first, count = parts[item]
+        return leg(f, k, item, lambda c: pl.ds(c * nb + first, count), held, ms, mr)
+
+    def m_pass(k, item):
+        if k > 0:
+            arrive(m_legs, k - 1, item)
+        if k < n_z - 1:
+            launch(m_legs, k, item)
+
+    m_pass(0, 0)
+    m_pass(0, 1)
 
     def keep_own():
         orecv[ow] = held[pl.ds(z * nb + ow * per, per)]
     when_worker(ow, keep_own)
 
-    def work():
+    def begin():
         for copy in o_copies:
             copy.wait_recv()
         for p in range(per):
             pieces = [orecv[o, p].astype(F32) for o in range(n_ow)]
-            update = orthogonal(jnp.concatenate(pieces, axis=0))
+            work[p] = normalized(jnp.concatenate(pieces, axis=0))
+
+    def sweeps(count):
+        def run():
+            for p in range(per):
+                iterate = work[p]
+                for _ in range(count):
+                    iterate = sweep(iterate).astype(BF16)
+                work[p] = iterate
+        return run
+
+    def end():
+        for p in range(per):
+            advanced = sweep(work[p])
+            update = (math.sqrt(advanced.shape[0]) * advanced).astype(BF16)
             rows = update.shape[0] // n_ow
             for o in range(n_ow):
                 ubuf[o, p] = update[o * rows:(o + 1) * rows]
-    when_worker(ow, work)
+
+    before = (ITERS - 1) // 2
+    when_worker(ow, begin)
+    m_pass(1, 0)
+    when_worker(ow, sweeps(before))
+    m_pass(1, 1)
+    when_worker(ow, sweeps(ITERS - 1 - before))
+    when_worker(ow, end)
 
     home = pl.ds(dp * nb + ow * per, per)
     u_copies = []
@@ -183,8 +241,36 @@
         every[home] = ubuf[ow]
     when_worker(ow, keep_update)
 
-    for copy in m_copies:
-        copy.wait_recv()
+    for k in range(2, n_z - 1):
+        for item in range(2):
+            m_pass(k, item)
+
+    for t in range(1, n_ow):
+        when_worker(owner_from(t), u_copies[t - 1].wait_recv)
+
+    def v_region(item):
+        first, count = parts[0] if item == 0 else parts[1]
+        side = 1 - y if item == 2 else y
+        return lambda c: pl.ds((2 * c + side) * nb + first, count)
+
+    def v_legs(f, k, item):
+        return leg(f, k, item, v_region(item), every, vs, vr)
+
+    b_own = every.at[v_region(1)(z)]
+    b_copy = remote(b_own, b_own, bs, br, (other, ow))
+    b_copy.start()
+    launch(v_legs, 0, 0)
+    launch(v_legs, 0, 1)
+
+    def across(chunk, sem):
+        piece = every.at[v_region(0)(chunk)]
+        return remote(piece, piece, ws.at[sem], wr.at[sem], (other, ow))
+
+    a_copies = [(across(z, 2 * (n_z - 1)), None)]
+    a_copies[0][0].start()
+
+    m_pass(n_z - 1, 0)
+    m_pass(n_z - 1, 1)
 
     def place_of(m):
         m = jnp.maximum(m, 0)
@@ -197,31 +283,23 @@
     q_copy = remote(ysel, yselrecv, qs, qr, (other, ow))
     q_copy.start()
 
-    for t in range(1, n_ow):
-        when_worker(owner_from(t), u_copies[t - 1].wait_recv)
-
-    def chunk(g):
-        return pl.ds(g * nb, nb)
-
-    v_copies = []
-    for t in range(n_z - 1):
-        copy = remote(
-            every.at[chunk(dp)], every.at[chunk(dp)], vs.at[t], vr.at[t], (2 * up(t) + y, ow)
-        )
-        copy.start()
-        v_copies.append(copy)
-    w_copies = []
-    copy = remote(
-        every.at[chunk(dp)], every.at[chunk(dp)], ws.at[n_z - 1], wr.at[n_z - 1], (other, ow)
-    )
-    copy.start()
-    w_copies.append(copy)
-    for t in range(n_z - 1):
-        v_copies[t].wait_recv()
-        g = 2 * down(t) + y
-        copy = remote(every.at[chunk(g)], every.at[chunk(g)], ws.at[t], wr.at[t], (other, ow))
-        copy.start()
-        w_copies.append(copy)
+    b_copy.wait_recv()
+    launch(v_legs, 0, 2)
+
+    def v_pass(k):
+        for item in range(3):
+            arrive(v_legs, k - 1, item)
+            if k < n_z - 1:
+                launch(v_legs, k, item)
+            if item == 0:
+                for f in range(2):
+                    chunk = z - flows[f][0] * k
+                    copy = across(chunk, 2 * (k - 1) + f)
+                    pl.when(within(chunk))(copy.start)
+                    a_copies.append((copy, within(chunk)))
+
+    for k in range(1, n_z - 1):
+        v_pass(k)
 
     q_copy.wait_recv()
 
@@ -237,12 +315,18 @@
         return carry
     lax.fori_loop(0, n_slots, renew, 0)
 
-    for copy in w_copies:
-        copy.wait_recv()
+    v_pass(n_z - 1)
+    for copy, there in a_copies:
+        if there is None:
+            copy.wait_recv()
+        else:
+            pl.when(there)(copy.wait_recv)
     upd_ref[...] = every[...]
 
-    for copy in y_copies + z_copies + m_copies + [q_copy] + v_copies + w_copies:
+    for copy in y_copies + z_copies + [q_copy, b_copy, a_copies[0][0]]:
         copy.wait_send()
+    for copy, sent in pending + a_copies[1:]:
+        pl.when(sent)(copy.wait_send)
     for t in range(1, n_ow):
         when_worker(owner_at(t), o_copies[t - 1].wait_send)
         when_worker(ow, u_copies[t - 1].wait_send)
@@ -258,10 +342,13 @@
     block = (rows, cols)
     vmem = pl.BlockSpec(memory_space=pltpu.VMEM)
     dma = pltpu.SemaphoreType.DMA
-    counts = (n_z, n_z - 1, n_ow - 1, n_z - 1, None, n_ow - 1, n_z - 1, n_z)
+    hops = n_z - 1
+    counts = (
+        (n_z,), (hops,), (n_ow - 1,), (2, hops, 2), (), (n_ow - 1,), (2, hops, 3), (2 * hops + 1,), ()
+    )
     sems = []
     for count in counts:
-        sems += [dma if count is None else dma((count,))] * 2
+        sems += [dma(count) if count else dma] * 2
     updates, renewed = pl.pallas_call(
         functools.partial(kernel, n_dp, n_ow, per, workers),
         out_shape=(
@@ -278,6 +365,7 @@
             pltpu.VMEM((nb,) + block, F32),
             pltpu.VMEM((n_z * nb,) + block, BF16),
             pltpu.VMEM((n_ow, per) + block, BF16),
+            pltpu.VMEM((per, n_ow * rows, cols), BF16),
             pltpu.VMEM((n_ow, per) + block, BF16),
             pltpu.VMEM((mats,) + block, BF16),
             pltpu.VMEM((n_slots,) + block, BF16),

time: 59 us -> 57 us (0.966); the launches traced: 58 us -> 56.9 us
  Pallas kernels: 54.2 us -> 53.1 us
    pallas_call x1, Pallas kernels: 54.2 us -> 53.1 us  [local(): pl.pallas_call(functools.partial(kernel, n_dp, n_ow, per, workers), out_s...]
where the time goes in v2:
time: 57 us; the launch traced here: 56.9 us
  Pallas kernels  53.1 us (93%)
  local copies, waits for them, and re-layouts  3.16 us (6%)
  between operations  0.65 us (1%)
    pallas_call x1, Pallas kernels, local(): pl.pallas_call(functools.partial(kernel, n_dp, n_ow, per, workers), out_s...  53.1 us
    unnamed x4, local copies, waits for them, and re-layouts  3.16 us

profile of v2, /device:TPU:0, one launch (start us, length us, event | category | flops | bytes accessed | tf_op | source)
XLA Modules:
  0.0 56.9 jit_solution(11888441239685943787)
XLA Ops:
  0.6 53.1 %shard_map.50 = (bf16[32,128,128]{2,1,0:T(8,128)(2,1)}, f32[8,128,128]{2,1,0:T(8,128)}) custom-call(s32[64]{0:T(128)} %slots_ref.1, f32[32,128,128]{2,1,0:T(8,128)} %bitcast.1, f32[8,128,128]{2,1,0:T(8,128)} %mom_ref.1), custom_call_target="tpu_custom_call" | custom-call | tf_op jit(solution)/shard_map/pallas_call | solution.py:352
  53.7 0.0 copy-start
  53.7 2.4 %copy.7 = bf16[32,128,128]{2,1,0:T(8,128)(2,1)} copy(bf16[32,128,128]{2,1,0:T(8,128)(2,1)} %get-tuple-element.4) | data formatting | bytes 2097152
  56.1 0.0 copy-done
  56.1 0.8 %copy.8 = f32[8,128,128]{2,1,0:T(8,128)} copy(f32[8,128,128]{2,1,0:T(8,128)S(1)} %copy-done) | data formatting | bytes 1048576
Async XLA Ops:
  53.7 2.4 %copy-start = (f32[8,128,128]{2,1,0:T(8,128)S(1)}, f32[8,128,128]{2,1,0:T(8,128)}, u32[]{:S(2)}) copy-start(f32[8,128,128]{2,1,0:T(8,128)} %get-tuple-element.5) | copy-start | bytes 1572868

commit v3 on v2

--- a/solution.py
+++ b/solution.py
@@ -269,6 +269,9 @@
     a_copies = [(across(z, 2 * (n_z - 1)), None)]
     a_copies[0][0].start()
 
+    b_copy.wait_recv()
+    launch(v_legs, 0, 2)
+
     m_pass(n_z - 1, 0)
     m_pass(n_z - 1, 1)
 
@@ -283,8 +286,6 @@
     q_copy = remote(ysel, yselrecv, qs, qr, (other, ow))
     q_copy.start()
 
-    b_copy.wait_recv()
-    launch(v_legs, 0, 2)
 
     def v_pass(k):
         for item in range(3):

time: 57 us -> 57 us (level)
  no operation moved by 1% of the time
where the time goes in v3:
time: 57 us; the launch traced here: 56.9 us
  Pallas kernels  53.1 us (93%)
  local copies, waits for them, and re-layouts  3.16 us (6%)
  between operations  0.65 us (1%)
    pallas_call x1, Pallas kernels, local(): pl.pallas_call(functools.partial(kernel, n_dp, n_ow, per, workers), out_s...  53.1 us
    unnamed x4, local copies, waits for them, and re-layouts  3.16 us

profile of v3, /device:TPU:0, one launch (start us, length us, event | category | flops | bytes accessed | tf_op | source)
XLA Modules:
  0.0 56.9 jit_solution(9566846811501603077)
XLA Ops:
  0.6 53.1 %shard_map.50 = (bf16[32,128,128]{2,1,0:T(8,128)(2,1)}, f32[8,128,128]{2,1,0:T(8,128)}) custom-call(s32[64]{0:T(128)} %slots_ref.1, f32[32,128,128]{2,1,0:T(8,128)} %bitcast.1, f32[8,128,128]{2,1,0:T(8,128)} %mom_ref.1), custom_call_target="tpu_custom_call" | custom-call | tf_op jit(solution)/shard_map/pallas_call | solution.py:353
  53.7 0.0 copy-start
  53.7 2.4 %copy.7 = bf16[32,128,128]{2,1,0:T(8,128)(2,1)} copy(bf16[32,128,128]{2,1,0:T(8,128)(2,1)} %get-tuple-element.4) | data formatting | bytes 2097152
  56.1 0.0 copy-done
  56.1 0.8 %copy.8 = f32[8,128,128]{2,1,0:T(8,128)} copy(f32[8,128,128]{2,1,0:T(8,128)S(1)} %copy-done) | data formatting | bytes 1048576
Async XLA Ops:
  53.7 2.4 %copy-start = (f32[8,128,128]{2,1,0:T(8,128)S(1)}, f32[8,128,128]{2,1,0:T(8,128)}, u32[]{:S(2)}) copy-start(f32[8,128,128]{2,1,0:T(8,128)} %get-tuple-element.5) | copy-start | bytes 1572868
